TPU v7x, 1024 devices: a whole 4x4x32 slice. The times are simulated.
1024 devices in a mesh: grp: 16 (over z_hi, y), sp: 16 (over z_lo, core), tp: 4 (over x).
Axes of the slice: x: 4, y: 4, z: 32 (z_hi: 4, z_lo: 8; z = z_hi * 8 + z_lo), core: 2. Of those that a mesh axis runs over, the one named last changes fastest.
Arguments:
- queries: bfloat16 [16, 3072, 2560], P('grp', 'sp', 'tp'), may hold values from -60 to 60
- key_tokens: bfloat16 [16, 3072, 2560], P('grp', 'sp', 'tp'), may hold values from -60 to 60
- value_tokens: bfloat16 [16, 3072, 2560], P('grp', 'sp', 'tp'), may hold values from -6 to 6
- norm_gains: float32 [2, 2560], P(None, 'grp'), may hold values from 0.25 to 1.75
- lengths: int32 [16], P('grp'), may hold values from 768 to 3072
Outputs:
- attended: bfloat16 [16, 3072, 2560], P('grp', 'sp', 'tp')
All inputs are finite; a program needn't handle non-finite values.
Results may differ from a plain program's by a relative error of at most 0.011.
Values may be sent and summed in bfloat16 or wider, within the bound.
A program may use at most 64 MiB of HBM per device.

v0:
```python
import math

import jax
import jax.numpy as jnp
from jax import lax
from jax.sharding import PartitionSpec as P

HEAD_DIM = 128


EPSILON = 1e-06
MASKED = -1e30


def in_order(parts, dim):
    parts = jnp.moveaxis(parts, 0, dim)
    lengths = parts.shape
    return parts.reshape(*lengths[:dim], lengths[dim] * lengths[dim + 1], *lengths[dim + 2 :])


def copy_for_each(shard, axis):
    copies = jnp.broadcast_to(shard, (lax.axis_size(axis), *shard.shape))
    return lax.all_to_all(copies, axis, split_axis=0, concat_axis=0, tiled=True)


def gather_directly(shard, axis, dim):
    return in_order(copy_for_each(shard, axis), dim)


def sent_together(arrays, axis, dim, along):
    ends, at = ([], 0)
    for a in arrays[:-1]:
        at += a.shape[along]
        ends.append(at)
    both = jnp.concatenate(arrays, axis=along)
    return tuple(jnp.split(lax.all_gather(both, axis, axis=dim, tiled=True), ends, axis=along))


def attend_block(running, query_heads, key_piece, value_piece, length):
    largest, denominator, numerator = running
    row_count = key_piece.shape[0]
    heads_here = query_heads.shape[1]
    key_heads = key_piece.reshape(row_count, heads_here, HEAD_DIM)
    value_heads = value_piece.reshape(row_count, heads_here, HEAD_DIM)
    scores = jnp.einsum(
        "qhd,khd->hqk", query_heads, key_heads, preferred_element_type=jnp.float32
    ) * (1.0 / math.sqrt(HEAD_DIM))
    visible = jnp.arange(row_count, dtype=jnp.int32) < length
    scores = jnp.where(visible[None, None, :], scores, MASKED)
    newest = jnp.maximum(largest, jnp.max(scores, axis=-1))
    weights = jnp.where(visible[None, None, :], jnp.exp(scores - newest[:, :, None]), 0.0)
    factor = jnp.exp(largest - newest)
    denominator = jnp.sum(weights, axis=-1)
    update = jnp.einsum(
        "hqk,khd->qhd",
        weights.astype(jnp.bfloat16),
        value_heads,
        preferred_element_type=jnp.float32,
    )
    numerator = numerator * factor.T[:, :, None] + update
    return (newest, denominator, numerator)


def per_device(queries, key_tokens, value_tokens, norm_gains, lengths):
    query_rows = queries[0]
    key_rows = key_tokens[0]
    value_rows = value_tokens[0]
    length = lengths[0]
    query_wide = query_rows.astype(jnp.float32)
    key_wide = key_rows.astype(jnp.float32)
    query_square, key_square = lax.psum(
        (jnp.sum(query_wide * query_wide, axis=1), jnp.sum(key_wide * key_wide, axis=1)), "tp"
    )
    gathered_gains = gather_directly(norm_gains, "grp", 1)
    local_width = query_rows.shape[1]
    full_width = local_width * lax.axis_size("tp")
    local_gains = lax.dynamic_slice_in_dim(
        gathered_gains, lax.axis_index("tp") * local_width, local_width, 1
    )
    query_norm = (
        query_wide * lax.rsqrt(query_square / full_width + EPSILON)[:, None] * local_gains[0]
    ).astype(jnp.bfloat16)
    key_norm = (
        key_wide * lax.rsqrt(key_square / full_width + EPSILON)[:, None] * local_gains[1]
    ).astype(jnp.bfloat16)
    tokens_here = query_rows.shape[0]
    heads_here = local_width // HEAD_DIM
    query_heads = query_norm.reshape(tokens_here, heads_here, HEAD_DIM)
    initial = (
        jnp.full((heads_here, tokens_here), MASKED, jnp.float32),
        jnp.zeros((heads_here, tokens_here), jnp.float32),
        jnp.zeros((tokens_here, heads_here, HEAD_DIM), jnp.float32),
    )
    pieces = sent_together((key_norm, value_rows), "sp", 0, 1)
    final_state = lax.cond(
        jnp.int32(0) < length,
        lambda current: attend_block(current, query_heads, pieces[0], pieces[1], length),
        lambda current: current,
        initial,
    )
    result = final_state[2] / final_state[1].T[:, :, None]
    return result.reshape(tokens_here, local_width).astype(jnp.bfloat16)[None]


def solution(mesh):
    placed = (
        P("grp", "sp", "tp"),
        P("grp", "sp", "tp"),
        P("grp", "sp", "tp"),
        P(None, "grp"),
        P("grp"),
    )
    return jax.shard_map(
        per_device, mesh=mesh, in_specs=placed, out_specs=P("grp", "sp", "tp"), check_vma=False
    )
```

profile of v0, /device:TPU:2, one launch (start us, length us, event | category | flops | bytes accessed | tf_op | source)
XLA Modules:
  0.0 213.7 jit_solution(17501769425316495183)
XLA Ops:
  6.5 1.3 broadcast_in_dim.41
  7.8 31.1 %all-to-all-start = ((f32[16,2,160]{2,1,0:T(2,128)}), f32[16,2,160]{2,1,0:T(2,128)S(1)}, u32[]{:S(2)}, u32[]{:S(2)}) async-start(f32[16,2,160]{2,1,0:T(2,128)} %broadcast_in_dim.41), calls=%async_computation | async-start | bytes 65536 | tf_op jit(solution)/shard_map/all_to_all | solution.py:23
  38.9 0.0 all-gather.2.cloned.1.call-start
  39.0 1.1 multiply_reduce_fusion
  40.1 1.1 fusion.15
  41.1 8.6 %all-reduce = (f32[192]{0:T(256)S(1)}, f32[192]{0:T(256)S(1)}) all-reduce(f32[192]{0:T(256)S(1)} %fusion.15, f32[192]{0:T(256)S(1)} %multiply_reduce_fusion), channel_id=1, replica_groups=mesh['grp'=16,'sp'=16,'tp'=4] {'tp'}, use_global_device_ids=true, to_apply=%region_1.0 | all-reduce | flops 384 | bytes 3072 | tf_op jit(solution)/shard_map/psum | solution.py:71
  49.8 13.6 %all-to-all-done = f32[16,2,160]{2,1,0:T(2,128)S(1)} async-done(((f32[16,2,160]{2,1,0:T(2,128)}), f32[16,2,160]{2,1,0:T(2,128)S(1)}, u32[]{:S(2)}, u32[]{:S(2)}) %all-to-all-start) | async-done | bytes 20512 | tf_op jit(solution)/shard_map/all_to_all | solution.py:23
  63.4 0.1 reshape.50
  63.5 0.1 dynamic-slice_reduce_fusion
  63.6 1.1 fusion.17
  64.6 1.8 pad_maximum_fusion
  66.4 0.0 all-gather.2.cloned.1.call-update
  66.4 1.1 copy.25
  68.2 0.2 multiply_convert_fusion
  68.4 110.7 %all-gather.2.cloned.1.call-done = bf16[3072,1280]{1,0:T(8,128)(2,1)} async-done(((bf16[192,1280]{1,0:T(8,128)(2,1)}), bf16[3072,1280]{1,0:T(8,128)(2,1)}) %all-gather.2.cloned.1.call-update) | async-done | bytes 7864336 | tf_op jit(solution)/shard_map/all_gather | solution.py:36
  179.1 26.5 %conditional.1 = (f32[5,192]{1,0:T(8,128)S(1)}, f32[192,5,128]{2,0,1:T(8,128)S(1)}) conditional(s32[]{:T(128)} %convert_element_type.42, () %tuple.13, (s32[]{:T(128)}, bf16[3072,1280]{1,0:T(8,128)(2,1)}, bf16[192,5,128]{0,2,1:T(8,128)(2,1)S(1)}) %tuple.14), branch_computations={%region_4.0_spmd, %region_5.8_spmd} | conditional | flops 1548414976 | bytes 75491344 | solution.py:95
  179.1 0.7 iota_compare_fusion
  179.7 10.7 %copy.26 = bf16[3072,1280]{0,1:T(8,128)(2,1)} copy(bf16[3072,1280]{1,0:T(8,128)(2,1)} %get-tuple-element.28) | data formatting | bytes 15728640 | tf_op jit(solution)/shard_map
  190.4 4.9 %fusion.18 = (bf16[3072,640]{0,1:T(8,128)(2,1)}, bf16[3072,640]{0,1:T(8,128)(2,1)S(1)}) fusion(bf16[3072,1280]{0,1:T(8,128)(2,1)} %copy.26), kind=kLoop, calls=%fused_computation.28 | loop fusion | bytes 15728640 | tf_op jit(solution)/shard_map/split | solution.py:36
  195.3 2.3 %fusion = (f32[5,192]{1,0:T(8,128)S(1)}, f32[5,192,3072]{2,1,0:T(8,128)S(1)}) fusion(pred[3072]{0:T(1024)(128)(4,1)S(1)} %iota_compare_fusion, bf16[192,5,128]{0,2,1:T(8,128)(2,1)S(1)} %get-tuple-element.29, bf16[3072,5,128]{0,2,1:T(8,128)(2,1)S(1)} %bitcast.23), kind=kOutput, calls=%fused_computation.2 | convolution fusion | flops 763821120 | bytes 15981312 | tf_op jit(solution)/shard_map/cond/branch_1_fun/qhd,khd->hqk/dot_general | solution.py:45
  197.5 5.0 %fusion.9 = f32[192,5,128]{2,0,1:T(8,128)S(1)} fusion(bf16[3072,5,128]{0,2,1:T(8,128)(2,1)} %bitcast.24, f32[5,192,3072]{2,1,0:T(8,128)S(1)} %get-tuple-element.39, f32[5,192]{1,0:T(8,128)S(1)} %get-tuple-element.37, pred[3072]{0:T(1024)(128)(4,1)S(1)} %iota_compare_fusion, f32[192,5]{0,1:T(8,128)S(1)} %get-tuple-element.36), kind=kOutput, calls=%fused_computation.8 | convolution fusion | flops 769843200 | bytes 16230912 | tf_op jit(solution)/shard_map/cond/branch_1_fun/hqk,khd->qhd/dot_general | solution.py:54
  202.5 3.1 %fusion.2 = f32[5,192]{1,0:T(8,128)S(1)} fusion(f32[5,192,3072]{2,1,0:T(8,128)S(1)} %get-tuple-element.39, f32[5,192]{1,0:T(8,128)S(1)} %get-tuple-element.37, pred[3072]{0:T(1024)(128)(4,1)S(1)} %iota_compare_fusion), kind=kLoop, calls=%fused_computation.4 | loop fusion | flops 14744640 | bytes 11807232 | tf_op jit(solution)/shard_map/cond/branch_1_fun/reduce_sum | solution.py:53
  205.6 0.2 divide_convert_fusion
  205.8 0.2 copy.28
  206.0 0.9 copy.29
  (4 shorter events, 0.0 us)
Async XLA Ops:
  7.8 55.5 %all-to-all-start = ((f32[16,2,160]{2,1,0:T(2,128)}), f32[16,2,160]{2,1,0:T(2,128)S(1)}, u32[]{:S(2)}, u32[]{:S(2)}) async-start(f32[16,2,160]{2,1,0:T(2,128)} %broadcast_in_dim.41), calls=%async_computation | async-start | bytes 65536 | tf_op jit(solution)/shard_map/all_to_all | solution.py:23
  38.9 140.2 %all-gather.2.cloned.1.call-start = ((), (), s32[]{:S(2)}) async-start(), calls=%async_computation.1 | async-start | bytes 8355840 | tf_op jit(solution)/shard_map/all_gather | solution.py:36
Sparse Core Ops, SparseCore 0:
  66.6 112.4 all-gather.1
where the time goes:
time: 214 us
  waiting for transfers between devices  124 us (58%)
  starting transfers between devices  31.1 us (15%)
  local copies, waits for them, and re-layouts  19.2 us (9%)
  between operations  14.1 us (7%)
  other arithmetic  9.12 us (4%)
  blocking collectives  8.62 us (4%)
  matrix products  7.21 us (3%)
    all_gather x1, waiting for transfers between devices, sent_together(): lax.all_gather(both, axis, axis=dim, tiled=True)  111 us
    all_to_all x1, starting transfers between devices, copy_for_each(): return lax.all_to_all(copies, axis, split_axis=0, concat_axis=0, tiled=True)  31.1 us
    all_to_all x1, waiting for transfers between devices, copy_for_each(): return lax.all_to_all(copies, axis, split_axis=0, concat_axis=0, tiled=True)  13.6 us
    another operation x1, local copies, waits for them, and re-layouts  10.7 us
    psum x1, blocking collectives, per_device(): lax.psum((jnp.sum(query_wide * query_wide, axis=1), jnp.sum(key_wide * ke...  8.62 us
    dot_general x1, matrix products, attend_block(): jnp.einsum('hqk,khd->qhd', weights.astype(jnp.bfloat16), value_heads, pre...  4.96 us
    split x1, local copies, waits for them, and re-layouts, sent_together(): jnp.split(lax.all_gather(both, axis, axis=dim, tiled=True), ends, axis=al...  4.87 us
  transfers between devices with their start and end apart: 2, of which 2 were waited for; matrix products, arithmetic and copies ran while one was open for 2% of the time, Pallas kernels for 0%

commit v1 on v0

v1 whole, which is shorter than its diff:
```python
import functools
import math

import jax
import jax.numpy as jnp
from jax import lax
from jax.experimental import pallas as pl
from jax.experimental.pallas import tpu as pltpu
from jax.sharding import PartitionSpec as P

HEAD_DIM = 128
EPSILON = 1e-06
MASKED = -1e30
MESH = pl.DeviceIdType.MESH

OWNERS = (1, 2, 3, 5, 6)
HEAD_ORDER = (2, 0, 4, 1, 3)
CHIPS = 8


def near_to_far(chip):
    return sorted(range(CHIPS), key=lambda other: (abs(other - chip), other))


def pick(index, choices, default):
    value = jnp.int32(default)
    for key, choice in choices:
        value = jnp.where(index == key, jnp.int32(choice), value)
    return value


def attention_kernel(
    sizes,
    length_ref,
    q_ref,
    k_ref,
    v_ref,
    gains_ref,
    out_ref,
    q_buf,
    k_buf,
    v_buf,
    k_norm,
    scale_buf,
    part_buf,
    gains_buf,
    gain_row,
    score_ref,
    o_buf,
    send_q,
    send_k,
    send_v,
    send_s,
    send_p,
    send_g,
    send_f,
    send_o,
    recv_q,
    recv_k,
    recv_v,
    recv_s,
    recv_p,
    recv_g,
    recv_o,
):
    groups, tensors, full_width = sizes
    rows, width = q_ref.shape
    slices = gains_buf.shape[0]
    piece = gains_ref.shape[1]
    group = lax.axis_index("grp")
    me = lax.axis_index("sp")
    column = lax.axis_index("tp")
    chip = me // 2
    side = me % 2
    partner = me + 1 - 2 * side
    gives_gains = (group // slices) == column
    my_slice = group % slices
    owner = functools.reduce(jnp.logical_or, [chip == c for c in OWNERS])
    head = pick(chip, [(c, h) for h, c in enumerate(OWNERS)], 0)
    columns = pl.ds(pl.multiple_of(head * HEAD_DIM, HEAD_DIM), HEAD_DIM)

    barrier = pltpu.get_barrier_semaphore()
    for step in range(1, CHIPS):
        pl.semaphore_signal(
            barrier,
            inc=1,
            device_id={"sp": lax.rem(chip + step, CHIPS) * 2 + side},
            device_id_type=MESH,
        )
    pl.semaphore_signal(barrier, inc=1, device_id={"sp": partner}, device_id_type=MESH)
    for step in range(1, tensors):
        pl.semaphore_signal(
            barrier,
            inc=1,
            device_id={"tp": lax.rem(column + step, tensors)},
            device_id_type=MESH,
        )
    for y in range(slices):
        source = column * slices + y

        @pl.when(source != group)
        def _():
            pl.semaphore_signal(barrier, inc=1, device_id={"grp": source}, device_id_type=MESH)

    ones = jnp.ones((8, width), jnp.bfloat16)
    for place, ref in enumerate((q_ref, k_ref)):
        wide = ref[...].astype(jnp.float32)
        square = wide * wide
        high = square.astype(jnp.bfloat16)
        low = (square - high.astype(jnp.float32)).astype(jnp.bfloat16)
        over = (((1,), (1,)), ((), ()))
        total = lax.dot_general(ones, high, over, preferred_element_type=jnp.float32)
        total = total + lax.dot_general(ones, low, over, preferred_element_type=jnp.float32)
        part_buf[pl.ds(column, 1), pl.ds(place, 1), :] = total[None, 0:1, :]

    near = CHIPS - 1 + 1 + tensors - 1
    pl.semaphore_wait(barrier, near + jnp.where(gives_gains, groups - 1, 0))

    def block_copies(h):
        lanes = pl.ds(h * HEAD_DIM, HEAD_DIM)
        target = {"sp": OWNERS[h] * 2 + side}
        return [
            pltpu.make_async_remote_copy(
                src_ref=q_ref.at[:, lanes],
                dst_ref=q_buf.at[chip],
                send_sem=send_q.at[h],
                recv_sem=recv_q.at[chip],
                device_id=target,
                device_id_type=MESH,
            ),
            pltpu.make_async_remote_copy(
                src_ref=k_ref.at[:, lanes],
                dst_ref=k_buf.at[me],
                send_sem=send_k.at[h],
                recv_sem=recv_k.at[me],
                device_id=target,
                device_id_type=MESH,
            ),
            pltpu.make_async_remote_copy(
                src_ref=v_ref.at[:, lanes],
                dst_ref=v_buf.at[me],
                send_sem=send_v.at[h],
                recv_sem=recv_v.at[me],
                device_id=target,
                device_id_type=MESH,
            ),
        ]

    def scale_copy(h):
        return pltpu.make_async_remote_copy(
            src_ref=scale_buf.at[me],
            dst_ref=scale_buf.at[me],
            send_sem=send_s.at[h],
            recv_sem=recv_s.at[me],
            device_id={"sp": OWNERS[h] * 2 + side},
            device_id_type=MESH,
        )

    def part_copy(step):
        return pltpu.make_async_remote_copy(
            src_ref=part_buf.at[column],
            dst_ref=part_buf.at[column],
            send_sem=send_p.at[step],
            recv_sem=recv_p.at[column],
            device_id={"tp": lax.rem(column + step, tensors)},
            device_id_type=MESH,
        )

    def gain_copy(step):
        return pltpu.make_async_remote_copy(
            src_ref=gains_ref,
            dst_ref=gains_buf.at[my_slice],
            send_sem=send_g.at[step],
            recv_sem=recv_g.at[my_slice],
            device_id={"grp": lax.rem(group + step, groups)},
            device_id_type=MESH,
        )

    def forward_copies(block, k_from, v_from):
        trips = (
            (k_from, k_buf, recv_k),
            (v_from, v_buf, recv_v),
            (scale_buf.at[block], scale_buf, recv_s),
        )
        return [
            pltpu.make_async_remote_copy(
                src_ref=source,
                dst_ref=into.at[block],
                send_sem=send_f.at[place, block // 2],
                recv_sem=landing.at[block],
                device_id={"sp": partner},
                device_id_type=MESH,
            )
            for place, (source, into, landing) in enumerate(trips)
        ]

    for step in range(1, tensors):
        part_copy(step).start()

    @pl.when(gives_gains)
    def _():
        for step in range(1, groups):
            gain_copy(step).start()

    for h in HEAD_ORDER:

        @pl.when(chip != OWNERS[h])
        def _():
            for copy in block_copies(h):
                copy.start()

    for step in range(1, tensors):
        other = lax.rem(column + step, tensors)
        pltpu.make_async_remote_copy(
            src_ref=part_buf.at[column],
            dst_ref=part_buf.at[other],
            send_sem=send_p.at[step],
            recv_sem=recv_p.at[other],
            device_id={"tp": other},
            device_id_type=MESH,
        ).wait_recv()
    sums = part_buf[0]
    for t in range(1, tensors):
        sums = sums + part_buf[t]
    scale_buf[pl.ds(me, 1)] = lax.rsqrt(sums / full_width + EPSILON)[None]
    for h in HEAD_ORDER:

        @pl.when(chip != OWNERS[h])
        def _():
            scale_copy(h).start()

    def own_forwards():
        return forward_copies(me, k_ref.at[:, columns], v_ref.at[:, columns])

    def passed_forwards(block):
        return forward_copies(block, k_buf.at[block], v_buf.at[block])

    def scale_column(block, place):
        row = scale_buf[block][place : place + 1, :]
        diagonal = lax.broadcasted_iota(jnp.int32, (rows, rows), 0) == lax.broadcasted_iota(
            jnp.int32, (rows, rows), 1
        )
        spread = jnp.where(diagonal, jnp.broadcast_to(row, (rows, rows)), 0.0)
        return jnp.sum(spread, axis=1, keepdims=True)

    @pl.when(owner)
    def _():
        for copy in own_forwards():
            copy.start()

        q_buf[pl.ds(chip, 1)] = q_ref[:, columns][None]
        k_buf[pl.ds(me, 1)] = k_ref[:, columns][None]
        v_buf[pl.ds(me, 1)] = v_ref[:, columns][None]

    @pl.when(gives_gains)
    def _():
        gains_buf[pl.ds(my_slice, 1)] = gains_ref[...][None]

    for y in range(slices):
        source = column * slices + y

        @pl.when(source != group)
        def _():
            pltpu.make_async_remote_copy(
                src_ref=gains_ref,
                dst_ref=gains_buf.at[y],
                send_sem=send_g.at[0],
                recv_sem=recv_g.at[y],
                device_id={"grp": source},
                device_id_type=MESH,
            ).wait_recv()

    for y in range(slices):
        gain_row[:, y * piece : (y + 1) * piece] = gains_buf[y]

    @pl.when(owner)
    def _():
        gains = gain_row[:, columns]
        query_gain = gains[0:1, :]
        key_gain = gains[1:2, :]

        def normalize_key(block):
            wide = k_buf[block].astype(jnp.float32)
            k_norm[pl.ds(block, 1)] = (wide * scale_column(block, 1) * key_gain).astype(
                jnp.bfloat16
            )[None]

        def landed(block):
            for buf, sem in ((k_buf, recv_k), (v_buf, recv_v), (scale_buf, recv_s)):
                pltpu.make_async_remote_copy(
                    src_ref=buf.at[block],
                    dst_ref=buf.at[block],
                    send_sem=send_f.at[0, 0],
                    recv_sem=sem.at[block],
                    device_id={"sp": partner},
                    device_id_type=MESH,
                ).wait_recv()

        normalize_key(me)
        landed(partner)
        normalize_key(partner)

        order = pick(
            chip,
            [
                (c, sum(o * CHIPS**i for i, o in enumerate(near_to_far(c)[1:])))
                for c in OWNERS
            ],
            0,
        )

        def arrive(step, left):
            there = lax.rem(left, CHIPS)
            block = there * 2 + side
            landed(block)
            for copy in passed_forwards(block):
                copy.start()
            normalize_key(block)
            other = there * 2 + 1 - side
            landed(other)
            normalize_key(other)
            pltpu.make_async_remote_copy(
                src_ref=q_buf.at[there],
                dst_ref=q_buf.at[there],
                send_sem=send_q.at[0],
                recv_sem=recv_q.at[there],
                device_id={"sp": partner},
                device_id_type=MESH,
            ).wait_recv()
            return left // CHIPS

        lax.fori_loop(0, CHIPS - 1, arrive, order)

        length = length_ref[0]
        factor = math.log2(math.e) / math.sqrt(HEAD_DIM)
        span = 2 * rows

        def attend(there):
            wide = q_buf[there].astype(jnp.float32)
            query = (wide * scale_column(there * 2 + side, 0) * query_gain * factor).astype(
                jnp.bfloat16
            )
            best = None
            for c in range(CHIPS):
                keys = k_norm[2 * c : 2 * c + 2].reshape(span, HEAD_DIM)
                scores = lax.dot_general(
                    query, keys, (((1,), (1,)), ((), ())), preferred_element_type=jnp.float32
                )
                place = lax.broadcasted_iota(jnp.int32, (1, span), 1) + c * span
                scores = scores + jnp.where(place < length, 0.0, MASKED)
                score_ref[:, c * span : (c + 1) * span] = scores
                highest = jnp.max(scores, axis=1, keepdims=True)
                best = highest if best is None else jnp.maximum(best, highest)
            total = None
            numerator = None
            for c in range(CHIPS):
                weights = jnp.exp2(score_ref[:, c * span : (c + 1) * span] - best)
                part = jnp.sum(weights, axis=1, keepdims=True)
                values = v_buf[2 * c : 2 * c + 2].reshape(span, HEAD_DIM)
                update = jnp.dot(
                    weights.astype(jnp.bfloat16), values, preferred_element_type=jnp.float32
                )
                total = part if total is None else total + part
                numerator = update if numerator is None else numerator + update
            return (numerator / total).astype(jnp.bfloat16)

        def result_copy(there):
            return pltpu.make_async_remote_copy(
                src_ref=o_buf.at[there],
                dst_ref=out_ref.at[:, columns],
                send_sem=send_o.at[there],
                recv_sem=recv_o.at[head],
                device_id={"sp": there * 2 + side},
                device_id_type=MESH,
            )

        backward = pick(
            chip,
            [
                (c, sum(o * CHIPS**i for i, o in enumerate(near_to_far(c)[:0:-1])))
                for c in OWNERS
            ],
            0,
        )

        def answer(step, left):
            there = lax.rem(left, CHIPS)
            o_buf[pl.ds(there, 1)] = attend(there)[None]
            result_copy(there).start()
            return left // CHIPS

        lax.fori_loop(0, CHIPS - 1, answer, backward)
        out_ref[:, columns] = attend(chip)

        for step in range(1, CHIPS):
            result_copy(lax.rem(chip + step, CHIPS)).wait_send()
            for copy in passed_forwards(lax.rem(chip + step, CHIPS) * 2 + side):
                copy.wait_send()
        for copy in own_forwards():
            copy.wait_send()

    for h in HEAD_ORDER:

        @pl.when(chip != OWNERS[h])
        def _():
            for copy in block_copies(h):
                copy.wait_send()
            scale_copy(h).wait_send()
            lanes = pl.ds(h * HEAD_DIM, HEAD_DIM)
            pltpu.make_async_remote_copy(
                src_ref=out_ref.at[:, lanes],
                dst_ref=out_ref.at[:, lanes],
                send_sem=send_o.at[0],
                recv_sem=recv_o.at[h],
                device_id={"sp": OWNERS[h] * 2 + side},
                device_id_type=MESH,
            ).wait_recv()

    for step in range(1, tensors):
        part_copy(step).wait_send()

    @pl.when(gives_gains)
    def _():
        for step in range(1, groups):
            gain_copy(step).wait_send()


def per_device(sizes, queries, key_tokens, value_tokens, norm_gains, lengths):
    groups, tensors, _ = sizes
    rows, width = queries.shape[1:]
    heads = width // HEAD_DIM
    piece = norm_gains.shape[1]
    slices = width // piece
    blocks = 2 * CHIPS
    vmem = pl.BlockSpec(memory_space=pltpu.VMEM)
    dma = pltpu.SemaphoreType.DMA
    out = pl.pallas_call(
        functools.partial(attention_kernel, sizes),
        out_shape=jax.ShapeDtypeStruct((rows, width), jnp.bfloat16),
        in_specs=[pl.BlockSpec(memory_space=pltpu.SMEM)] + [vmem] * 4,
        out_specs=vmem,
        scratch_shapes=[
            pltpu.VMEM((CHIPS, rows, HEAD_DIM), jnp.bfloat16),
            pltpu.VMEM((blocks, rows, HEAD_DIM), jnp.bfloat16),
            pltpu.VMEM((blocks, rows, HEAD_DIM), jnp.bfloat16),
            pltpu.VMEM((blocks, rows, HEAD_DIM), jnp.bfloat16),
            pltpu.VMEM((blocks, 2, rows), jnp.float32),
            pltpu.VMEM((tensors, 2, rows), jnp.float32),
            pltpu.VMEM((slices, 2, piece), jnp.float32),
            pltpu.VMEM((2, width), jnp.float32),
            pltpu.VMEM((rows, blocks * rows), jnp.float32),
            pltpu.VMEM((CHIPS, rows, HEAD_DIM), jnp.bfloat16),
            dma((heads,)),
            dma((heads,)),
            dma((heads,)),
            dma((heads,)),
            dma((max(tensors, 2),)),
            dma((max(groups, 2),)),
            dma((3, CHIPS)),
            dma((CHIPS,)),
            dma((CHIPS,)),
            dma((blocks,)),
            dma((blocks,)),
            dma((blocks,)),
            dma((max(tensors, 2),)),
            dma((slices,)),
            dma((heads,)),
        ],
        compiler_params=pltpu.CompilerParams(
            collective_id=0, has_side_effects=True, vmem_limit_bytes=48 * 1024 * 1024
        ),
    )(lengths, queries[0], key_tokens[0], value_tokens[0], norm_gains)
    return out[None]


def solution(mesh):
    placed = (
        P("grp", "sp", "tp"),
        P("grp", "sp", "tp"),
        P("grp", "sp", "tp"),
        P(None, "grp"),
        P("grp"),
    )
    groups, tensors = mesh.shape["grp"], mesh.shape["tp"]
    sizes = (groups, tensors, 5 * HEAD_DIM * tensors)
    return jax.shard_map(
        functools.partial(per_device, sizes),
        mesh=mesh,
        in_specs=placed,
        out_specs=P("grp", "sp", "tp"),
        check_vma=False,
    )
```

time: 214 us -> 95.5 us (0.45)
  the two profiles are of different devices: /device:TPU:2 before, /device:TPU:129 now
where the time goes in v1:
time: 95.5 us; the launch traced here: 95.2 us
  Pallas kernels  90.3 us (95%)
  local copies, waits for them, and re-layouts  4.2 us (4%)
    pallas_call x1, Pallas kernels, per_device(): pl.pallas_call(functools.partial(attention_kernel, sizes), out_shape=jax....  90.3 us
    unnamed x9, local copies, waits for them, and re-layouts  4.2 us

profile of v1, /device:TPU:129, one launch (start us, length us, event | category | flops | bytes accessed | tf_op | source)
XLA Modules:
  0.0 95.2 jit_solution(16769644316630194980)
XLA Ops:
  0.7 0.0 copy-start.3
  0.7 0.7 copy-done.3
  1.3 0.0 copy-start
  1.3 0.9 copy-done
  2.3 0.0 copy-start.1
  2.3 0.9 copy-done.1
  3.2 0.0 copy-start.2
  3.2 0.9 copy-done.2
  4.2 90.3 %shard_map.55 = bf16[192,640]{1,0:T(8,128)(2,1)S(1)} custom-call(s32[1]{0:T(128)S(6)} %copy.7.length_ref, bf16[192,640]{1,0:T(8,128)(2,1)S(1)} %bitcast.5, bf16[192,640]{1,0:T(8,128)(2,1)S(1)} %bitcast.6, bf16[192,640]{1,0:T(8,128)(2,1)S(1)} %bitcast.7, f32[2,160]{1,0:T(2,128)S(1)} %copy-done.3), custom_call_target="tpu_custom_call" | custom-call | tf_op jit(solution)/shard_map/pallas_call | solution.py:437
  94.5 0.7 copy.8
Async XLA Ops:
  0.7 0.7 copy-start.3
  1.3 0.9 copy-start
  2.3 0.9 copy-start.1
  3.2 0.9 copy-start.2
